TPU v7x, 32 devices: a whole 2x2x4 slice. The times are simulated.
32 devices in a mesh: dp: 4 (over y, core), expert: 8 (over z, x).
Axes of the slice: x: 2, y: 2, z: 4, core: 2. Of those that a mesh axis runs over, the one named last changes fastest.
Arguments:
- tokens: bfloat16 [4, 4, 4096, 1024], P('dp', None, 'expert'), may hold values from -8000 to 8000
- slot_params: bfloat16 [1024, 128], replicated, may hold values from -8 to 8
- dest: int32 [4, 4, 16], P('dp', None, 'expert'), may hold values from 0 to 63, as said below
- lengths: int32 [4, 4], P('dp'), may hold values from 256 to 4096
- w_in: bfloat16 [64, 1024, 4096], P('expert', None, 'dp'), may hold values from -0.1875 to 0.1875
- w_out: bfloat16 [64, 4096, 1024], P('expert', 'dp'), may hold values from -3 to 3
Outputs:
- mixed: bfloat16 [4, 64, 256, 1024], P('dp', 'expert')
Inputs may be any that keep to these rules, and one draw needn't show every extreme that they name: For each g, dest[g] holds every number of 0 to 63 once; the 8 blocks held by one device (block indices j from k * 2 on, for every q) go to output blocks of different devices, device d holding output blocks d * 4 * 2 onward, so each device receives at most one block from each device.
All inputs are finite; a program needn't handle non-finite values.
Results may differ from a plain program's by a relative error of at most 0.01.
Values may be sent and summed in bfloat16 or wider, within the bound.
A program may use at most 128 MiB of HBM per device.

v0:
```python
import jax
import jax.numpy as jnp
from jax import lax
from jax.sharding import PartitionSpec as P


def arrange(labels, wanted):
    matches = labels[None, :] == jnp.arange(wanted, dtype=jnp.int32)[:, None]
    senders = jnp.arange(labels.shape[0], dtype=jnp.int32)[None, :]
    return jnp.sum(jnp.where(matches, senders, 0), axis=1)


def local(tokens, slot_params, dest, lengths, w_in, w_out):
    seq_count = tokens.shape[1]
    blocks_here = dest.shape[2]
    width = tokens.shape[3]
    block_tokens = tokens.shape[2] // blocks_here
    held_blocks = seq_count * blocks_here
    shard_count = lax.axis_size("expert")
    shard_index = lax.axis_index("expert")
    block_total = blocks_here * shard_count
    slots_total = slot_params.shape[1]
    owned_slots = slots_total // shard_count
    block_local = tokens.reshape(held_blocks, block_tokens, width)
    targets = dest.reshape(held_blocks)
    ordinal = jnp.arange(held_blocks, dtype=jnp.int32)
    source_ids = (
        ordinal // blocks_here * block_total + shard_index * blocks_here + ordinal % blocks_here
    )
    peer_device = targets // held_blocks
    dest_slot = targets % held_blocks
    seq_lengths = lengths[0]
    seq_of = source_ids // block_total
    place_of = source_ids % block_total
    member = seq_of[:, None] == jnp.arange(seq_count, dtype=jnp.int32)[None, :]
    length_of = jnp.sum(jnp.where(member, seq_lengths[None, :], 0), axis=1)
    token_place = (
        place_of[:, None] * block_tokens + jnp.arange(block_tokens, dtype=jnp.int32)[None, :]
    )
    live_mask = token_place < length_of[:, None]
    logits = jnp.dot(
        block_local.reshape(held_blocks * block_tokens, width),
        slot_params,
        preferred_element_type=jnp.float32,
    )
    logits = logits.reshape(held_blocks, block_tokens, slots_total)
    masked = jnp.where(live_mask[..., None], logits, -jnp.inf)
    block_top = jnp.max(masked, axis=1)
    seq_top = jnp.max(jnp.where(member[:, :, None], block_top[:, None, :], -jnp.inf), axis=0)
    top = lax.pmax(seq_top, "expert")
    block_ref = jnp.sum(jnp.where(member[:, :, None], top[None, :, :], 0.0), axis=1)
    weight = jnp.where(live_mask[..., None], jnp.exp(logits - block_ref[:, None, :]), 0.0)
    block_mass = jnp.sum(weight, axis=1)
    seq_mass = jnp.sum(jnp.where(member[:, :, None], block_mass[:, None, :], 0.0), axis=0)
    block_numer = jnp.einsum(
        "bts,btd->bsd", weight.astype(jnp.bfloat16), block_local, preferred_element_type=jnp.float32
    )
    seq_numer = jnp.einsum(
        "bq,bsd->qsd", member.astype(jnp.float32), block_numer, precision=lax.Precision.HIGHEST
    )
    numer_own = lax.psum_scatter(seq_numer, "expert", scatter_dimension=1, tiled=True)
    mass_own = lax.psum_scatter(seq_mass, "expert", scatter_dimension=1, tiled=True)
    slot_in = (numer_own / mass_own[..., None]).astype(jnp.bfloat16)
    gathered = lax.all_gather(slot_in, "dp", axis=0, tiled=True)
    experts_here = w_in.shape[0]
    per_expert = owned_slots // experts_here
    grouped = gathered.reshape(gathered.shape[0], experts_here, per_expert, width)
    hidden = jax.nn.gelu(
        jnp.einsum("nepd,edh->neph", grouped, w_in, preferred_element_type=jnp.float32)
    ).astype(jnp.bfloat16)
    result = jnp.einsum("neph,ehd->nepd", hidden, w_out, preferred_element_type=jnp.float32)
    slot_out = lax.psum_scatter(
        result.reshape(seq_count * lax.axis_size("dp"), owned_slots, width),
        "dp",
        scatter_dimension=0,
        tiled=True,
    ).astype(jnp.bfloat16)
    mix = jax.nn.softmax(logits, axis=-1).astype(jnp.bfloat16)
    chosen = lax.all_gather(slot_out, "expert", axis=1, tiled=True)[seq_of]
    combined = jnp.einsum("bts,bsd->btd", mix, chosen, preferred_element_type=jnp.float32)
    finished = jnp.where(live_mask[..., None], combined, 0.0).astype(jnp.bfloat16)
    outgoing = (
        jnp.zeros((shard_count, block_tokens, width), jnp.bfloat16).at[peer_device].set(finished)
    )
    labels = jnp.full((shard_count,), -1, jnp.int32).at[peer_device].set(dest_slot)
    arrived, arrived_labels = (
        lax.all_to_all(outgoing, "expert", split_axis=0, concat_axis=0, tiled=True),
        lax.all_to_all(labels, "expert", split_axis=0, concat_axis=0, tiled=True),
    )
    result = arrived[arrange(arrived_labels, held_blocks)]
    return result.reshape(1, held_blocks, block_tokens, width)


def solution(mesh):
    return jax.shard_map(
        local,
        mesh=mesh,
        in_specs=(
            P("dp", None, "expert", None),
            P(),
            P("dp", None, "expert"),
            P("dp", None),
            P("expert", None, "dp"),
            P("expert", "dp", None),
        ),
        out_specs=P("dp", "expert", None, None),
        check_vma=False,
    )
```

profile of v0, /device:TPU:0, one launch (start us, length us, event | category | flops | bytes accessed | tf_op | source)
XLA Modules:
  0.0 423.0 jit_solution(3697806245935985554)
XLA Ops:
  6.6 0.8 select_reduce_fusion.5
  7.5 3.1 select_reduce_fusion
  10.7 23.1 %pmax.7 = f32[4,128]{1,0:T(4,128)S(1)} all-reduce(f32[4,128]{1,0:T(4,128)S(1)} %select_reduce_fusion.3), channel_id=1, replica_groups=mesh['dp'=4,'expert'=8] {'expert'}, use_global_device_ids=true, to_apply=%region_5.6 | all-reduce | flops 512 | bytes 4096 | tf_op jit(solution)/shard_map/pmax | solution.py:50
  33.9 0.4 fusion.22
  34.3 0.7 copy.53
  35.2 3.1 fusion.24
  38.2 5.6 %fusion.5 = f32[4,128,1024]{2,0,1:T(4,128)} fusion(f32[8,128,1024]{2,1,0:T(8,128)S(1)} %fusion.24, s32[8]{0:T(128)S(1)} %get-tuple-element.7), kind=kOutput, calls=%fused_computation.10 | convolution fusion | flops 50331680 | bytes 6291488 | tf_op jit(solution)/shard_map/bq,bsd->qsd/dot_general | solution.py:58
  43.9 0.6 dynamic-slice
  45.2 49.9 %reduce-scatter.7.cloned.1.call-done = f32[16,4]{1,0:T(8,128)} async-done(((f32[128,4]{1,0:T(8,128)}), f32[16,4]{1,0:T(8,128)}) %reduce-scatter.7.cloned.1.call-update) | async-done | bytes 272
  95.0 105.0 %all-reduce.3.cloned.1.call-done = f32[4,128,1024]{2,0,1:T(4,128)} async-done(((f32[4,128,1024]{2,0,1:T(4,128)}), f32[4,128,1024]{2,0,1:T(4,128)}) %all-reduce.3.cloned.1.call-update) | async-done | bytes 2097168
  200.0 1.1 fusion.32
  201.2 7.3 %all_gather.6 = bf16[16,16,1024]{2,1,0:T(8,128)(2,1)S(1)} all-gather(bf16[4,16,1024]{2,1,0:T(8,128)(2,1)S(1)} %copy.45), channel_id=1, replica_groups=mesh['dp'=4,'expert'=8] {'dp'}, dimensions={0}, use_global_device_ids=true | all-gather | bytes 655360 | tf_op jit(solution)/shard_map/all_gather | solution.py:64
  208.5 0.3 copy.46
  208.8 8.9 %fusion.19 = bf16[16,8,2,1024]{3,0,2,1:T(8,128)(2,1)S(1)} fusion(bf16[16,8,2,1024]{3,0,2,1:T(8,128)(2,1)S(1)} %bitcast.55, bf16[8,1024,1024]{2,1,0:T(8,128)(2,1)} %param.10), kind=kOutput, calls=%fused_computation.23 | convolution fusion | flops 539230208 | bytes 17825792 | tf_op jit(solution)/shard_map/nepd,edh->neph/dot_general | solution.py:69
  217.7 8.8 %fusion.1 = f32[8,16,2,1024]{3,1,2,0:T(8,128)S(1)} fusion(bf16[16,8,2,1024]{3,0,2,1:T(8,128)(2,1)S(1)} %fusion.19, bf16[8,1024,1024]{2,1,0:T(8,128)(2,1)} %param.11), kind=kOutput, calls=%fused_computation.5 | convolution fusion | flops 536870912 | bytes 18350080 | tf_op jit(solution)/shard_map/neph,ehd->nepd/dot_general | solution.py:71
  226.4 1.6 copy.47
  228.1 23.7 %reduce-scatter.5.cloned.1.call-done = f32[4,16,1024]{2,1,0:T(8,128)} async-done(((f32[16,16,1024]{2,1,0:T(8,128)}), f32[4,16,1024]{2,1,0:T(8,128)}) %reduce-scatter.5.cloned.1.call-update) | async-done | bytes 262160 | tf_op jit(solution)/shard_map/reduce_scatter | solution.py:72
  251.9 1.6 convert_element_type.23
  253.8 0.6 scatter_custom_fusion.1
  254.4 0.7 copy.49
  255.1 5.5 %all-to-all-start.1 = ((s32[8,1,1]{2,1,0:T(1,128)}), s32[8,1,1]{2,1,0:T(1,128)S(1)}, u32[]{:S(2)}, u32[]{:S(2)}) async-start(s32[8,1,1]{2,1,0:T(1,128)} %copy.49), calls=%async_computation.2 | async-start | bytes 8192 | tf_op jit(solution)/shard_map/all_to_all | solution.py:88
  260.6 0.6 fusion.49
  261.3 32.9 %all-gather.2.cloned.1.call-done = bf16[4,128,1024]{2,1,0:T(8,128)(2,1)} async-done(((bf16[4,16,1024]{2,1,0:T(8,128)(2,1)}), bf16[4,128,1024]{2,1,0:T(8,128)(2,1)}) %all-gather.2.cloned.1.call-update) | async-done | bytes 1048592 | tf_op jit(solution)/shard_map/all_gather | solution.py:79
  294.2 1.9 gather_fusion
  296.1 5.6 %select_convert_fusion = bf16[8,256,1024]{2,1,0:T(8,128)(2,1)} fusion(pred[8,256]{1,0:T(8,128)(4,1)S(1)} %add_compare_fusion, bf16[8,128,1024]{2,1,0:T(8,128)(2,1)S(1)} %gather_fusion, f32[8,256]{1,0:T(8,128)S(1)} %fusion.49, f32[8,256,128]{2,1,0:T(8,128)S(1)} %get-tuple-element.6), kind=kOutput, calls=%fused_computation.9 | convolution fusion | flops 541853824 | bytes 7350272 | tf_op jit(solution)/shard_map/bts,bsd->btd/dot_general | solution.py:80
  301.7 2.5 broadcast_in_dim.131
  304.3 10.9 %scatter_fusion = bf16[8,256,1024]{2,1,0:T(8,128)(2,1)} fusion(bf16[8,256,1024]{2,1,0:T(8,128)(2,1)} %broadcast_in_dim.131, s32[8]{0:T(128)S(1)} %fusion.42, bf16[8,256,1024]{2,1,0:T(8,128)(2,1)} %select_convert_fusion), kind=kCustom, calls=%fused_computation.2 | custom fusion | bytes 12582944 | tf_op jit(solution)/shard_map/scatter | solution.py:83
  315.1 4.5 %all-to-all-start = ((bf16[8,256,1024]{2,1,0:T(8,128)(2,1)}), bf16[8,256,1024]{2,1,0:T(8,128)(2,1)}, u32[]{:S(2)}, u32[]{:S(2)}) async-start(bf16[8,256,1024]{2,1,0:T(8,128)(2,1)} %scatter_fusion), calls=%async_computation.1 | async-start | bytes 8388608 | tf_op jit(solution)/shard_map/all_to_all | solution.py:87
  319.7 0.2 reduce
  319.9 0.1 select_reduce_fusion.4
  320.1 91.4 %all-to-all-done = bf16[8,256,1024]{2,1,0:T(8,128)(2,1)} async-done(((bf16[8,256,1024]{2,1,0:T(8,128)(2,1)}), bf16[8,256,1024]{2,1,0:T(8,128)(2,1)}, u32[]{:S(2)}, u32[]{:S(2)}) %all-to-all-start) | async-done | bytes 4194336 | tf_op jit(solution)/shard_map/all_to_all | solution.py:87
  411.4 5.0 %gather_fusion.1 = bf16[8,256,1024]{2,1,0:T(8,128)(2,1)} fusion(bf16[8,256,1024]{2,1,0:T(8,128)(2,1)} %all-to-all-done, s32[1024]{0:T(1024)S(1)} %pad_clamp_fusion), kind=kCustom, calls=%fused_computation.1 | custom fusion | bytes 8388640 | tf_op jit(solution)/shard_map/gather | solution.py:90
  (33 shorter events, 1.0 us)
Async XLA Ops:
  6.5 1.0 copy-start
  6.5 88.5 %reduce-scatter.7.cloned.1.call-start = ((), (), s32[]{:S(2)}) async-start(), calls=%async_computation.6 | async-start | bytes 73728
  35.1 164.9 %all-reduce.3.cloned.1.call-start = ((), (), s32[]{:S(2)}) async-start(), calls=%async_computation.7 | async-start | bytes 4194304
  38.2 5.7 %copy-start.3 = (u32[32]{0:T(128)S(1)}, u32[32]{0:T(128)}, u32[]{:S(2)}) copy-start(u32[32]{0:T(128)} %constant.105) | copy-start | bytes 388
  43.9 208.0 %reduce-scatter.5.cloned.1.call-start = ((), (), s32[]{:S(2)}) async-start(), calls=%async_computation.4 | async-start | bytes 1310720 | tf_op jit(solution)/shard_map/reduce_scatter | solution.py:72
  217.7 35.8 %copy-start.2 = (s32[1,4,2]{1,2,0:T(2,128)S(1)}, s32[1,4,2]{1,2,0:T(2,128)}, u32[]{:S(2)}) copy-start(s32[1,4,2]{1,2,0:T(2,128)} %param.8) | copy-start | bytes 100
  228.1 66.1 %all-gather.2.cloned.1.call-start = ((), (), s32[]{:S(2)}) async-start(), calls=%async_computation.5 | async-start | bytes 1179648 | tf_op jit(solution)/shard_map/all_gather | solution.py:79
  255.1 60.0 %all-to-all-start.1 = ((s32[8,1,1]{2,1,0:T(1,128)}), s32[8,1,1]{2,1,0:T(1,128)S(1)}, u32[]{:S(2)}, u32[]{:S(2)}) async-start(s32[8,1,1]{2,1,0:T(1,128)} %copy.49), calls=%async_computation.2 | async-start | bytes 8192 | tf_op jit(solution)/shard_map/all_to_all | solution.py:88
  315.1 96.3 %all-to-all-start = ((bf16[8,256,1024]{2,1,0:T(8,128)(2,1)}), bf16[8,256,1024]{2,1,0:T(8,128)(2,1)}, u32[]{:S(2)}, u32[]{:S(2)}) async-start(bf16[8,256,1024]{2,1,0:T(8,128)(2,1)} %scatter_fusion), calls=%async_computation.1 | async-start | bytes 8388608 | tf_op jit(solution)/shard_map/all_to_all | solution.py:87
  320.0 96.4 %copy-start.1 = (bf16[1024,128]{1,0:T(8,128)(2,1)S(1)}, bf16[1024,128]{1,0:T(8,128)(2,1)}, u32[]{:S(2)}) copy-start(bf16[1024,128]{1,0:T(8,128)(2,1)} %param.7) | copy-start | bytes 786436
Sparse Core Ops, SparseCore 0:
  35.2 59.7 reduce-scatter.6
  98.6 101.3 all-reduce.2
  228.2 23.6 reduce-scatter.4
  253.9 40.2 all-gather.1
where the time goes:
time: 424 us; the launch traced here: 423 us
  waiting for transfers between devices  303 us (71%)
  matrix products  35 us (8%)
  blocking collectives  30.5 us (7%)
  local copies, waits for them, and re-layouts  25.2 us (6%)
  between operations  13.9 us (3%)
  starting transfers between devices  10.2 us (2%)
  other arithmetic  5.24 us (1%)
    unnamed x6, waiting for transfers between devices  155 us
    all_to_all x1, waiting for transfers between devices, local(): lax.all_to_all(outgoing, 'expert', split_axis=0, concat_axis=0, tiled=True)  91.4 us
    all_gather x1, waiting for transfers between devices, local(): chosen = lax.all_gather(slot_out, 'expert', axis=1, tiled=True)[seq_of]  32.9 us
    reduce_scatter x1, waiting for transfers between devices, local(): lax.psum_scatter(result.reshape(seq_count * lax.axis_size('dp'), owned_sl...  23.7 us
    pmax x1, blocking collectives, local(): top = lax.pmax(seq_top, 'expert')  23.1 us
    scatter x1, local copies, waits for them, and re-layouts, local(): jnp.zeros((shard_count, block_tokens, width), jnp.bfloat16).at[peer_device]  10.9 us
    dot_general x1, matrix products, local(): jnp.einsum('nepd,edh->neph', grouped, w_in, preferred_element_type=jnp.fl...  8.87 us
    dot_general x1, matrix products, local(): jnp.einsum('neph,ehd->nepd', hidden, w_out, preferred_element_type=jnp.fl...  8.76 us
  transfers between devices with their start and end apart: 6, of which 5 were waited for; matrix products, arithmetic and copies ran while one was open for 8% of the time, Pallas kernels for 0%

commit v1 on v0

v1 whole, which is shorter than its diff:
```python
import functools

import jax
import jax.numpy as jnp
from jax import lax
from jax.experimental import pallas as pl
from jax.experimental.pallas import tpu as pltpu
from jax.sharding import PartitionSpec as P

LANES = 128
FLOOR = -3.0e38
GATHER_BYTES = 512 * 1024


def pieces(value):
    high = lax.reduce_precision(value, 8, 7)
    rest = value - high
    middle = lax.reduce_precision(rest, 8, 7)
    return [high, middle, rest - middle]


def combine_kernel(order, seq_of, mix_ref, *refs):
    out_ref = refs[-1]
    start = 0
    for ref in refs[:-1]:
        shards, _, owned, columns = ref.shape
        outputs = ref[...].reshape(shards * owned, columns)
        out_ref[0, :, start : start + columns] = jnp.dot(
            mix_ref[0], outputs, preferred_element_type=jnp.float32
        ).astype(out_ref.dtype)
        start += columns


def combine(order, seq_of, mixes, outputs, held_blocks, block_tokens):
    slots_total = mixes.shape[2]
    width = sum(part.shape[3] for part in outputs)
    specs = [
        pl.BlockSpec((1, block_tokens, slots_total), lambda o, order, seq: (order[o], 0, 0))
    ]
    for part in outputs:
        specs.append(
            pl.BlockSpec(
                (part.shape[0], 1, part.shape[2], part.shape[3]),
                lambda o, order, seq: (0, seq[o], 0, 0),
            )
        )
    return pl.pallas_call(
        combine_kernel,
        grid_spec=pltpu.PrefetchScalarGridSpec(
            num_scalar_prefetch=2,
            grid=(held_blocks,),
            in_specs=specs,
            out_specs=pl.BlockSpec((1, block_tokens, width), lambda o, order, seq: (o, 0, 0)),
        ),
        out_shape=jax.ShapeDtypeStruct((held_blocks, block_tokens, width), jnp.bfloat16),
    )(order, seq_of, mixes, *outputs)


def local(tokens, slot_params, dest, lengths, w_in, w_out):
    seq_count = tokens.shape[1]
    tokens_here = tokens.shape[2]
    width = tokens.shape[3]
    blocks_here = dest.shape[2]
    block_tokens = tokens_here // blocks_here
    held_blocks = seq_count * blocks_here
    shard_count = lax.axis_size("expert")
    group_count = lax.axis_size("dp")
    shard_index = lax.axis_index("expert")
    slots_total = slot_params.shape[1]
    owned_slots = slots_total // shard_count
    feats = tokens[0]
    place = shard_index * tokens_here + jnp.arange(tokens_here, dtype=jnp.int32)
    live = (place[None, :] < lengths[0][:, None])[..., None]

    logits = jnp.dot(
        feats.reshape(seq_count * tokens_here, width),
        slot_params,
        preferred_element_type=jnp.float32,
    ).reshape(seq_count, tokens_here, slots_total)

    top = jnp.maximum(jnp.max(jnp.where(live, logits, -jnp.inf), axis=1), FLOOR)
    weight = jnp.where(live, jnp.exp(logits - top[:, None, :]), 0.0)
    mass = jnp.sum(weight, axis=1)
    numer = jnp.einsum(
        "qts,qtd->qsd", weight.astype(jnp.bfloat16), feats, preferred_element_type=jnp.float32
    ).astype(jnp.bfloat16)
    extra = jnp.stack(pieces(top) + pieces(mass), axis=-1).astype(jnp.bfloat16)
    extra = jnp.pad(extra, ((0, 0), (0, 0), (0, LANES - extra.shape[-1])))
    packed = jnp.concatenate([numer, extra], axis=-1)
    packed = packed.reshape(seq_count, shard_count, owned_slots, width + LANES)
    packed = lax.all_to_all(packed.transpose(1, 0, 2, 3), "expert", 0, 0, tiled=True)
    stats = packed[..., width : width + 6].astype(jnp.float32)
    tops = stats[..., 0] + stats[..., 1] + stats[..., 2]
    masses = stats[..., 3] + stats[..., 4] + stats[..., 5]
    scale = jnp.exp(tops - jnp.max(tops, axis=0, keepdims=True))
    mass_own = jnp.sum(scale * masses, axis=0)
    numer_own = jnp.sum(scale[..., None] * packed[..., :width].astype(jnp.float32), axis=0)
    slot_in = (numer_own / mass_own[..., None]).astype(jnp.bfloat16)

    mix = jnp.where(live, jax.nn.softmax(logits, axis=-1), 0.0).astype(jnp.bfloat16)
    mix = mix.reshape(held_blocks, block_tokens, slots_total)
    targets = dest.reshape(held_blocks)
    ordinal = jnp.arange(held_blocks, dtype=jnp.int32)
    shards = jnp.arange(shard_count, dtype=jnp.int32)
    goes = (targets // held_blocks)[None, :] == shards[:, None]
    pick = jnp.sum(jnp.where(goes, ordinal[None, :], 0), axis=1)
    label = jnp.sum(jnp.where(goes, (targets % held_blocks + 1)[None, :], 0), axis=1) - 1
    sender_seq = pick // blocks_here
    note = jnp.stack([label, sender_seq], axis=-1).astype(jnp.bfloat16)
    note = jnp.pad(note, ((0, 0), (0, slots_total - 2)))
    note = jnp.broadcast_to(note[:, None, :], (shard_count, 16, slots_total))
    outgoing = jnp.concatenate([mix[pick], note], axis=1)
    mixes = lax.all_to_all(outgoing, "expert", 0, 0, tiled=True)
    labels = mixes[:, block_tokens, 0].astype(jnp.int32)
    seqs = mixes[:, block_tokens, 1].astype(jnp.int32)
    comes = labels[None, :] == ordinal[:, None]
    order = jnp.sum(jnp.where(comes, shards[None, :], 0), axis=1)
    order_seq = jnp.sum(jnp.where(comes, seqs[None, :], 0), axis=1)

    gathered = lax.all_gather(slot_in, "dp", axis=0, tiled=True)
    experts_here = w_in.shape[0]
    per_expert = owned_slots // experts_here
    grouped = gathered.reshape(gathered.shape[0], experts_here, per_expert, width)
    hidden = jax.nn.gelu(
        jnp.einsum("nepd,edh->neph", grouped, w_in, preferred_element_type=jnp.float32)
    ).astype(jnp.bfloat16)
    result = jnp.einsum("neph,ehd->nepd", hidden, w_out, preferred_element_type=jnp.float32)
    partial = result.astype(jnp.bfloat16).reshape(
        group_count, seq_count, owned_slots, width
    )
    partial = lax.all_to_all(partial, "dp", 0, 0, tiled=True)
    slot_out = jnp.sum(partial.astype(jnp.float32), axis=0).astype(jnp.bfloat16)

    chunks = 1
    while seq_count * slots_total * width * 2 // chunks > GATHER_BYTES:
        chunks *= 2
    step = width // chunks
    outputs = [
        lax.all_gather(slot_out[..., c * step : (c + 1) * step], "expert", axis=0)
        for c in range(chunks)
    ]
    mixed = combine(order, order_seq, mixes, outputs, held_blocks, block_tokens)
    return mixed[None]


def solution(mesh):
    return jax.shard_map(
        local,
        mesh=mesh,
        in_specs=(
            P("dp", None, "expert", None),
            P(),
            P("dp", None, "expert"),
            P("dp", None),
            P("expert", None, "dp"),
            P("expert", "dp", None),
        ),
        out_specs=P("dp", "expert", None, None),
        check_vma=False,
    )
```

time: 424 us -> 165 us (0.39)
  waiting for transfers between devices: 303 us -> 29.5 us
  blocking collectives: 30.5 us -> 74.4 us
  local copies, waits for them, and re-layouts: 25.2 us -> 5.8 us
  between operations: 13.9 us -> 0.26 us
  matrix products: 35 us -> 22.3 us
  Pallas kernels: 0 us -> 7.74 us
  starting transfers between devices: 10.2 us -> 14.9 us
    unnamed x6 -> x0, waiting for transfers between devices: 155 us -> none
    all_gather x0 -> x2, blocking collectives: none -> 67.2 us  [local(): lax.all_gather(slot_out[..., c * step:(c + 1) * step], 'expert', axis=0)]
    all_to_all x2 -> x3, waiting for transfers between devices: 91.4 us -> 29.5 us  [the longest x1 22.7 us: local(): lax.all_to_all(packed.transpose(1, 0, 2, 3), 'expert', 0, 0, tiled=True)]
    all_gather x1 -> x0, waiting for transfers between devices: 32.9 us -> none  [local(): chosen = lax.all_gather(slot_out, 'expert', axis=1, tiled=True)[seq_of]]
    reduce_scatter x1 -> x0, waiting for transfers between devices: 23.7 us -> none  [local(): lax.psum_scatter(result.reshape(seq_count * lax.axis_size('dp'), owned_sl...]
    pmax x1 -> x0, blocking collectives: 23.1 us -> none  [local(): top = lax.pmax(seq_top, 'expert')]
    dot_general x4 -> x2, matrix products: 17.4 us -> 4.73 us  [the longest x1 3.28 us: local(): jnp.dot(feats.reshape(seq_count * tokens_here, width), slot_params, prefe...]
    scatter x2 -> x0, local copies, waits for them, and re-layouts: 11.4 us -> none  [the longest x1 10.9 us: local(): jnp.zeros((shard_count, block_tokens, width), jnp.bfloat16).at[peer_device]]
  transfers between devices with their start and end apart: 6 -> 3, of which waited for: 5 -> 2; matrix products, arithmetic and copies ran while one was open for 8% -> 18% of each run, Pallas kernels for 0% -> 0%
where the time goes in v1:
time: 165 us; the launch traced here: 164 us
  blocking collectives  74.4 us (45%)
  waiting for transfers between devices  29.5 us (18%)
  matrix products  22.3 us (14%)
  starting transfers between devices  14.9 us (9%)
  other arithmetic  8.99 us (5%)
  Pallas kernels  7.74 us (5%)
  local copies, waits for them, and re-layouts  5.8 us (4%)
    all_gather x2, blocking collectives, local(): lax.all_gather(slot_out[..., c * step:(c + 1) * step], 'expert', axis=0)  67.2 us
    all_to_all x1, waiting for transfers between devices, local(): lax.all_to_all(packed.transpose(1, 0, 2, 3), 'expert', 0, 0, tiled=True)  22.7 us
    dot_general x1, matrix products, local(): jnp.einsum('nepd,edh->neph', grouped, w_in, preferred_element_type=jnp.fl...  8.87 us
    dot_general x1, matrix products, local(): jnp.einsum('neph,ehd->nepd', hidden, w_out, preferred_element_type=jnp.fl...  8.75 us
    pallas_call x1, Pallas kernels, combine(): pl.pallas_call(combine_kernel, grid_spec=pltpu.PrefetchScalarGridSpec(num...  7.74 us
    all_to_all x1, starting transfers between devices, local(): lax.all_to_all(packed.transpose(1, 0, 2, 3), 'expert', 0, 0, tiled=True)  7.28 us
    all_gather x1, blocking collectives, local(): gathered = lax.all_gather(slot_in, 'dp', axis=0, tiled=True)  7.2 us
    all_to_all x1, waiting for transfers between devices, local(): partial = lax.all_to_all(partial, 'dp', 0, 0, tiled=True)  6.8 us
  transfers between devices with their start and end apart: 3, of which 2 were waited for; matrix products, arithmetic and copies ran while one was open for 18% of the time, Pallas kernels for 0%

profile of v1, /device:TPU:0, one launch (start us, length us, event | category | flops | bytes accessed | tf_op | source)
XLA Modules:
  0.0 164.0 jit_solution(8727506583473723285)
XLA Ops:
  0.0 0.8 broadcast_compare_fusion
  0.8 0.2 copy-done
  1.0 3.3 %select_reduce_fusion = (f32[4,128]{1,0:T(4,128)S(1)}, f32[4,512,128]{2,1,0:T(8,128)S(1)}) fusion(pred[4,512]{1,0:T(4,128)(4,1)S(1)} %broadcast_compare_fusion, bf16[1024,128]{1,0:T(8,128)(2,1)S(1)} %copy-done, bf16[1,4,512,1024]{3,2,1,0:T(8,128)(2,1)} %param.6), kind=kOutput, calls=%fused_computation.36 | convolution fusion | flops 537394688 | bytes 5509120 | tf_op jit(solution)/shard_map/dot_general | solution.py:75
  4.3 0.4 fusion.39
  4.6 1.4 fusion.11
  6.2 0.2 copy.38
  6.5 1.1 copy.59
  7.6 7.3 %all-to-all-start.1 = ((bf16[8,4,16,1152]{3,2,1,0:T(8,128)(2,1)}), bf16[8,4,16,1152]{3,2,1,0:T(8,128)(2,1)S(1)}, u32[]{:S(2)}, u32[]{:S(2)}) async-start(bf16[8,4,16,1152]{3,2,1,0:T(8,128)(2,1)} %bitcast.109), calls=%async_computation.1 | async-start | bytes 2359296 | tf_op jit(solution)/shard_map/all_to_all | solution.py:91
  15.4 3.9 %fusion.24 = bf16[4,512,128]{2,1,0:T(8,128)(2,1)S(1)} fusion(pred[4,512]{1,0:T(4,128)(4,1)S(1)} %broadcast_compare_fusion, f32[4,512,128]{2,1,0:T(8,128)S(1)} %get-tuple-element.20), kind=kOutput, calls=%fused_computation.22 | output fusion | flops 1052926 | bytes 1574912 | tf_op jit(solution)/shard_map/div | solution.py:100
  19.3 0.7 gather_fusion
  19.9 0.8 pad_maximum_fusion
  20.8 22.7 %all-to-all-done.1 = bf16[8,4,16,1152]{3,2,1,0:T(8,128)(2,1)S(1)} async-done(((bf16[8,4,16,1152]{3,2,1,0:T(8,128)(2,1)}), bf16[8,4,16,1152]{3,2,1,0:T(8,128)(2,1)S(1)}, u32[]{:S(2)}, u32[]{:S(2)}) %all-to-all-start.1) | async-done | bytes 1179680 | tf_op jit(solution)/shard_map/all_to_all | solution.py:91
  43.5 4.2 %all-to-all-start = ((bf16[8,272,128]{2,1,0:T(8,128)(2,1)}), bf16[8,272,128]{2,1,0:T(8,128)(2,1)}, u32[]{:S(2)}, u32[]{:S(2)}) async-start(bf16[8,272,128]{2,1,0:T(8,128)(2,1)} %pad_maximum_fusion), calls=%async_computation | async-start | bytes 1114112 | tf_op jit(solution)/shard_map/all_to_all | solution.py:113
  47.7 0.3 copy.54
  48.1 0.3 multiply_reduce_fusion
  48.4 0.8 copy.52
  49.3 0.2 broadcast_divide_fusion
  49.5 0.6 copy.43
  50.0 7.2 %all_gather.15 = bf16[16,16,1024]{2,1,0:T(8,128)(2,1)S(1)} all-gather(bf16[4,16,1024]{2,1,0:T(8,128)(2,1)S(1)} %copy.43), channel_id=1, replica_groups=mesh['dp'=4,'expert'=8] {'dp'}, dimensions={0}, use_global_device_ids=true | all-gather | bytes 655360 | tf_op jit(solution)/shard_map/all_gather | solution.py:120
  57.2 0.3 copy.44
  57.5 8.9 %fusion.36 = bf16[16,8,2,1024]{3,0,2,1:T(8,128)(2,1)S(1)} fusion(bf16[16,8,2,1024]{3,0,2,1:T(8,128)(2,1)S(1)} %bitcast.118, bf16[8,1024,1024]{2,1,0:T(8,128)(2,1)} %param.10), kind=kOutput, calls=%fused_computation.33 | convolution fusion | flops 539230208 | bytes 17825792 | tf_op jit(solution)/shard_map/nepd,edh->neph/dot_general | solution.py:125
  66.4 8.7 %fusion.25 = bf16[16,8,2,1024]{3,0,2,1:T(8,128)(2,1)S(1)} fusion(bf16[16,8,2,1024]{3,0,2,1:T(8,128)(2,1)S(1)} %fusion.36, bf16[8,1024,1024]{2,1,0:T(8,128)(2,1)} %param.11), kind=kOutput, calls=%fused_computation.23 | convolution fusion | flops 537133056 | bytes 17825792 | tf_op jit(solution)/shard_map/neph,ehd->nepd/dot_general | solution.py:127
  75.2 0.2 reshape.255
  75.4 1.0 copy.45
  76.4 3.5 %all-to-all-start.2 = ((bf16[4,4,16,1024]{3,1,2,0:T(4,128)(2,1)}), bf16[4,4,16,1024]{3,1,2,0:T(4,128)(2,1)S(1)}, u32[]{:S(2)}, u32[]{:S(2)}) async-start(bf16[4,4,16,1024]{3,1,2,0:T(4,128)(2,1)} %copy.45), calls=%async_computation.2 | async-start | bytes 1048576 | tf_op jit(solution)/shard_map/all_to_all | solution.py:131
  79.8 1.2 fusion.50
  81.1 0.7 select_reduce_fusion.1
  81.8 6.8 %all-to-all-done.2 = bf16[4,4,16,1024]{3,1,2,0:T(4,128)(2,1)S(1)} async-done(((bf16[4,4,16,1024]{3,1,2,0:T(4,128)(2,1)}), bf16[4,4,16,1024]{3,1,2,0:T(4,128)(2,1)S(1)}, u32[]{:S(2)}, u32[]{:S(2)}) %all-to-all-start.2) | async-done | bytes 524320 | tf_op jit(solution)/shard_map/all_to_all | solution.py:131
  88.6 0.3 reduce_sum.98
  89.0 33.8 %all-gather = bf16[32,16,512]{2,1,0:T(8,128)(2,1)} all-gather(bf16[4,16,512]{2,1,0:T(8,128)(2,1)S(1)} %copy.47), channel_id=2, replica_groups=mesh['dp'=4,'expert'=8] {'expert'}, dimensions={0}, use_global_device_ids=true | all-gather | bytes 589824 | tf_op jit(solution)/shard_map/all_gather | solution.py:139
  122.8 33.4 %all-gather.1 = bf16[32,16,512]{2,1,0:T(8,128)(2,1)} all-gather(bf16[4,16,512]{2,1,0:T(8,128)(2,1)S(1)} %copy.48), channel_id=3, replica_groups=mesh['dp'=4,'expert'=8] {'expert'}, dimensions={0}, use_global_device_ids=true | all-gather | bytes 589824 | tf_op jit(solution)/shard_map/all_gather | solution.py:139
  156.3 7.7 %shard_map.64 = bf16[8,256,1024]{2,1,0:T(8,128)(2,1)} custom-call(s32[8]{0:T(128)} %get-tuple-element.8.order, s32[8]{0:T(128)} %get-tuple-element.7.seq_of, bf16[8,272,128]{2,1,0:T(8,128)(2,1)} %all-to-all-done.mix_ref, bf16[8,4,16,512]{3,2,1,0:T(8,128)(2,1)} %bitcast.116, bf16[8,4,16,512]{3,2,1,0:T(8,128)(2,1)} %bitcast.117), custom_call_target="tpu_custom_call" | custom-call | tf_op jit(solution)/shard_map/pallas_call | solution.py:47
  (36 shorter events, 0.9 us)
Async XLA Ops:
  0.0 1.0 copy-start
  1.0 3.7 %copy-start.1 = (bf16[1,4,512,1024]{3,2,1,0:T(8,128)(2,1)S(1)}, bf16[1,4,512,1024]{3,2,1,0:T(8,128)(2,1)}, u32[]{:S(2)}) copy-start(bf16[1,4,512,1024]{3,2,1,0:T(8,128)(2,1)} %param.6) | copy-start | bytes 12582916
  6.5 8.4 %copy-start.2 = (s32[1,4,2]{1,2,0:T(2,128)S(1)}, s32[1,4,2]{1,2,0:T(2,128)}, u32[]{:S(2)}) copy-start(s32[1,4,2]{1,2,0:T(2,128)} %param.8) | copy-start | bytes 100
  7.6 35.9 %all-to-all-start.1 = ((bf16[8,4,16,1152]{3,2,1,0:T(8,128)(2,1)}), bf16[8,4,16,1152]{3,2,1,0:T(8,128)(2,1)S(1)}, u32[]{:S(2)}, u32[]{:S(2)}) async-start(bf16[8,4,16,1152]{3,2,1,0:T(8,128)(2,1)} %bitcast.109), calls=%async_computation.1 | async-start | bytes 2359296 | tf_op jit(solution)/shard_map/all_to_all | solution.py:91
  43.5 32.9 %all-to-all-start = ((bf16[8,272,128]{2,1,0:T(8,128)(2,1)}), bf16[8,272,128]{2,1,0:T(8,128)(2,1)}, u32[]{:S(2)}, u32[]{:S(2)}) async-start(bf16[8,272,128]{2,1,0:T(8,128)(2,1)} %pad_maximum_fusion), calls=%async_computation | async-start | bytes 1114112 | tf_op jit(solution)/shard_map/all_to_all | solution.py:113
  76.4 12.3 %all-to-all-start.2 = ((bf16[4,4,16,1024]{3,1,2,0:T(4,128)(2,1)}), bf16[4,4,16,1024]{3,1,2,0:T(4,128)(2,1)S(1)}, u32[]{:S(2)}, u32[]{:S(2)}) async-start(bf16[4,4,16,1024]{3,1,2,0:T(4,128)(2,1)} %copy.45), calls=%async_computation.2 | async-start | bytes 1048576 | tf_op jit(solution)/shard_map/all_to_all | solution.py:131
